TPU v7x, 256 devices: a whole 4x4x8 slice. The times are simulated.
256 devices in a mesh: row: 32 (over x, z_hi, core), col: 8 (over z_lo, y).
Axes of the slice: x: 4, y: 4, z: 8 (z_hi: 4, z_lo: 2; z = z_hi * 2 + z_lo), core: 2. Of those that a mesh axis runs over, the one named last changes fastest.
Arguments:
- amplitudes: float32 [32, 8, 1024, 1024], P('row', 'col'), may hold values from -6 to 6
- panels_left: bfloat16 [32, 2, 1024, 1024], P('row', None, 'col'), may hold values from -6 to 6
- panels_right: bfloat16 [8, 2, 1024, 1024], P('col', None, 'row'), may hold values from -6 to 6
- weights_right: bfloat16 [2, 8, 1024, 1024], P(None, 'col', 'row'), may hold values from -0.125 to 0.125
- weights_left: bfloat16 [2, 32, 1024, 1024], P(None, 'row', 'col'), may hold values from -0.125 to 0.125
- energy_left: float32 [32], P('row'), may hold values from -2 to -0.5
- energy_right: float32 [8], P('col'), may hold values from -2 to -0.5
- energy_virtual: float32 [1024], replicated, may hold values from 0.5 to 3
Outputs:
- updated: float32 [32, 8, 1024, 1024], P('row', 'col')
All inputs are finite; a program needn't handle non-finite values.
Results may differ from a plain program's by a relative error of at most 0.0018.
Values may be sent and summed in bfloat16 or wider, within the bound.
A program may use at most 128 MiB of HBM per device.

v0:
```python
import jax
import jax.numpy as jnp
from jax import lax
from jax.sharding import PartitionSpec as P


def combine_blocks(blocks):
    as_float = blocks.astype(jnp.float32)
    return (2.0 * as_float - jnp.swapaxes(as_float, -1, -2)).astype(jnp.bfloat16)


def body(
    amplitudes,
    panels_left,
    panels_right,
    weights_right,
    weights_left,
    energy_left,
    energy_right,
    energy_virtual,
):
    left_slab = panels_left[0]
    right_slab = panels_right[0]
    right_weight_slab = weights_right[:, 0]
    left_weight_slab = weights_left[:, 0]
    left_whole = lax.all_gather(left_slab, "col", axis=1, tiled=True)
    left_mixed = combine_blocks(left_whole)
    mixed_cols = left_mixed
    direct = jnp.einsum(
        "kac,kcb->ab",
        mixed_cols,
        lax.all_gather(right_weight_slab, "row", axis=1, tiled=True),
        preferred_element_type=jnp.float32,
    )
    right_whole = lax.all_gather(right_slab, "row", axis=1, tiled=True)
    right_mixed = combine_blocks(right_whole)
    mixed_cols = right_mixed
    mirror = jnp.einsum(
        "kac,kcb->ab",
        mixed_cols,
        lax.all_gather(left_weight_slab, "col", axis=1, tiled=True),
        preferred_element_type=jnp.float32,
    )
    residual = direct + jnp.transpose(mirror)
    virt_pair = energy_virtual[:, None] + energy_virtual[None, :]
    denominator = energy_left[0] + energy_right[0] - virt_pair
    return (amplitudes[0, 0] + residual / denominator)[None, None]


def solution(mesh):
    placed = (
        P("row", "col", None, None),
        P("row", None, "col", None),
        P("col", None, "row", None),
        P(None, "col", "row", None),
        P(None, "row", "col", None),
        P("row"),
        P("col"),
        P(),
    )
    return jax.shard_map(
        body, mesh=mesh, in_specs=placed, out_specs=P("row", "col", None, None), check_vma=False
    )
```

profile of v0, /device:TPU:1, one launch (start us, length us, event | category | flops | bytes accessed | tf_op | source)
XLA Modules:
  0.0 267.6 jit_solution(162221997629663721)
XLA Ops:
  6.5 0.0 all-gather.9.cloned.1.call-start
  6.5 0.7 all-gather.9.cloned.1.call-update
  7.3 0.0 all-gather.13.cloned.1.call-start
  7.3 0.7 all-gather.13.cloned.1.call-update
  8.0 0.0 all-gather.11.cloned.1.call-start
  8.1 0.7 all-gather.11.cloned.1.call-update
  8.7 0.0 all-gather.15.cloned.1.call-start
  8.8 0.5 all-gather.15.cloned.1.call-update
  10.6 57.3 %all-gather.9.cloned.1.call-done = bf16[1,2,1024,1024]{3,2,1,0:T(8,128)(2,1)} async-done(((bf16[1,2,128,1024]{3,2,1,0:T(8,128)(2,1)}), bf16[1,2,1024,1024]{3,2,1,0:T(8,128)(2,1)}) %all-gather.9.cloned.1.call-update) | async-done | bytes 4194320 | tf_op jit(solution)/shard_map/all_gather | solution.py:26
  68.0 6.5 %bitcast_convert_fusion.1 = f32[2,1024,1024]{2,1,0:T(8,128)} fusion(bf16[1,2,1024,1024]{3,2,1,0:T(8,128)(2,1)} %all-gather.9.cloned.1.call-done), kind=kLoop, calls=%fused_computation.13 | loop fusion | flops 2097152 | bytes 12582912 | tf_op jit(solution)/shard_map/convert_element_type | solution.py:8
  74.4 8.7 %copy.9 = f32[2,1024,1024]{1,2,0:T(8,128)} copy(f32[2,1024,1024]{2,1,0:T(8,128)} %bitcast_convert_fusion.1) | data formatting | bytes 16777216 | tf_op jit(solution)/shard_map/convert_element_type | solution.py:8
  83.1 47.2 %all-gather.13.cloned.1.call-done = bf16[1,2,1024,1024]{3,2,1,0:T(8,128)(2,1)} async-done(((bf16[1,2,32,1024]{3,2,1,0:T(8,128)(2,1)}), bf16[1,2,1024,1024]{3,2,1,0:T(8,128)(2,1)}) %all-gather.13.cloned.1.call-update) | async-done | bytes 4194320 | tf_op jit(solution)/shard_map/all_gather | solution.py:35
  130.2 6.5 %bitcast_convert_fusion = f32[2,1024,1024]{2,1,0:T(8,128)} fusion(bf16[1,2,1024,1024]{3,2,1,0:T(8,128)(2,1)} %all-gather.13.cloned.1.call-done), kind=kLoop, calls=%fused_computation.11 | loop fusion | flops 2097152 | bytes 12582912 | tf_op jit(solution)/shard_map/convert_element_type | solution.py:8
  136.7 8.7 %copy.12 = f32[2,1024,1024]{1,2,0:T(8,128)} copy(f32[2,1024,1024]{2,1,0:T(8,128)} %bitcast_convert_fusion) | data formatting | bytes 16777216 | tf_op jit(solution)/shard_map/convert_element_type | solution.py:8
  145.4 0.0 copy-start
  145.4 45.9 %all-gather.11.cloned.1.call-done = bf16[2,1,1024,1024]{3,2,0,1:T(8,128)(2,1)} async-done(((bf16[2,1,32,1024]{3,2,0,1:T(8,128)(2,1)}), bf16[2,1,1024,1024]{3,2,0,1:T(8,128)(2,1)}) %all-gather.11.cloned.1.call-update) | async-done | bytes 4194320 | tf_op jit(solution)/shard_map/all_gather | solution.py:32
  191.4 12.6 %fusion.2 = f32[1024,1024,1]{1,0,2:T(8,128)} fusion(f32[2,1024,1024]{1,2,0:T(8,128)} %copy.9, bf16[2,1,1024,1024]{3,2,0,1:T(8,128)(2,1)} %all-gather.11.cloned.1.call-done, bf16[1,2,1024,1024]{3,2,1,0:T(8,128)(2,1)} %all-gather.9.cloned.1.call-done), kind=kOutput, calls=%fused_computation.4 | convolution fusion | flops 4303355904 | bytes 20971520 | tf_op jit(solution)/shard_map/kac,kcb->ab/dot_general | solution.py:29
  204.0 41.8 %all-gather.15.cloned.1.call-done = bf16[2,1,1024,1024]{3,2,0,1:T(8,128)(2,1)} async-done(((bf16[2,1,128,1024]{3,2,0,1:T(8,128)(2,1)}), bf16[2,1,1024,1024]{3,2,0,1:T(8,128)(2,1)}) %all-gather.15.cloned.1.call-update) | async-done | bytes 4194320 | tf_op jit(solution)/shard_map/all_gather | solution.py:41
  245.8 0.0 copy-done
  245.8 15.3 %fusion.8 = f32[1,1,1024,1024]{3,2,1,0:T(8,128)} fusion(f32[1024,1024,1]{1,0,2:T(8,128)} %fusion.2, f32[1,1,1024,1024]{3,2,1,0:T(8,128)} %param.8, f32[1024]{0:T(1024)S(1)} %copy-done, f32[]{:T(128)} %bitcast.14, bf16[2,1,1024,1024]{3,2,0,1:T(8,128)(2,1)} %all-gather.15.cloned.1.call-done, f32[2,1024,1024]{1,2,0:T(8,128)} %copy.12, ...), kind=kOutput, calls=%fused_computation.9 | convolution fusion | flops 4308598784 | bytes 29364228 | tf_op jit(solution)/shard_map/kac,kcb->ab/dot_general | solution.py:38
Async XLA Ops:
  6.5 61.4 %all-gather.9.cloned.1.call-start = ((), (), s32[]{:S(2)}) async-start(), calls=%async_computation | async-start | bytes 4718592 | tf_op jit(solution)/shard_map/all_gather | solution.py:26
  7.3 123.0 %all-gather.13.cloned.1.call-start = ((), (), s32[]{:S(2)}) async-start(), calls=%async_computation.2 | async-start | bytes 4325376 | tf_op jit(solution)/shard_map/all_gather | solution.py:35
  8.0 183.4 %all-gather.11.cloned.1.call-start = ((), (), s32[]{:S(2)}) async-start(), calls=%async_computation.1 | async-start | bytes 4325376 | tf_op jit(solution)/shard_map/all_gather | solution.py:32
  8.7 237.0 %all-gather.15.cloned.1.call-start = ((), (), s32[]{:S(2)}) async-start(), calls=%async_computation.3 | async-start | bytes 4718592 | tf_op jit(solution)/shard_map/all_gather | solution.py:41
  145.4 100.3 %copy-start = (f32[1024]{0:T(1024)S(1)}, f32[1024]{0:T(1024)}, u32[]{:S(2)}) copy-start(f32[1024]{0:T(1024)} %param.15) | copy-start | bytes 12292
Sparse Core Ops, SparseCore 0:
  9.1 58.7 all-gather.8
  70.6 59.5 all-gather.12
  132.9 58.4 all-gather.10
  193.0 52.7 all-gather.14
where the time goes:
time: 268 us
  waiting for transfers between devices  195 us (73%)
  matrix products  27.9 us (10%)
  local copies, waits for them, and re-layouts  17.4 us (6%)
  between operations  14.4 us (5%)
  other arithmetic  12.9 us (5%)
    all_gather x1, waiting for transfers between devices, body(): left_whole = lax.all_gather(left_slab, 'col', axis=1, tiled=True)  57.3 us
    all_gather x1, waiting for transfers between devices, body(): right_whole = lax.all_gather(right_slab, 'row', axis=1, tiled=True)  47.2 us
    all_gather x1, waiting for transfers between devices, body(): lax.all_gather(right_weight_slab, 'row', axis=1, tiled=True)  45.9 us
    all_gather x1, waiting for transfers between devices, body(): lax.all_gather(left_weight_slab, 'col', axis=1, tiled=True)  41.8 us
    convert_element_type x2, local copies, waits for them, and re-layouts, combine_blocks(): as_float = blocks.astype(jnp.float32)  17.4 us
    dot_general x1, matrix products, body(): jnp.einsum('kac,kcb->ab', mixed_cols, lax.all_gather(left_weight_slab, 'c...  15.3 us
    convert_element_type x2, other arithmetic, combine_blocks(): as_float = blocks.astype(jnp.float32)  12.9 us
    dot_general x1, matrix products, body(): jnp.einsum('kac,kcb->ab', mixed_cols, lax.all_gather(right_weight_slab, '...  12.6 us
  transfers between devices with their start and end apart: 4, of which 4 were waited for; matrix products, arithmetic and copies ran while one was open for 16% of the time, Pallas kernels for 0%

commit v1 on v0

--- a/solution.py
+++ b/solution.py
@@ -23,7 +23,9 @@
     right_slab = panels_right[0]
     right_weight_slab = weights_right[:, 0]
     left_weight_slab = weights_left[:, 0]
-    left_whole = lax.all_gather(left_slab, "col", axis=1, tiled=True)
+    left_whole = jnp.concatenate(
+        lax.all_to_all(jnp.stack([left_slab] * lax.axis_size("col")), "col", 0, 0), axis=1
+    )
     left_mixed = combine_blocks(left_whole)
     mixed_cols = left_mixed
     direct = jnp.einsum(

time: 268 us -> 220 us (0.82)
  waiting for transfers between devices: 195 us -> 129 us
  other arithmetic: 12.9 us -> 23.2 us
  starting transfers between devices: 0.12 us -> 6.44 us
  local copies, waits for them, and re-layouts: 17.4 us -> 21 us
    all_to_all x0 -> x1, waiting for transfers between devices: none -> 65.3 us  [body(): lax.all_to_all(jnp.stack([left_slab] * lax.axis_size('col')), 'col', 0, 0)]
    all_gather x1 -> x0, waiting for transfers between devices: 57.3 us -> none  [body(): left_whole = lax.all_gather(left_slab, 'col', axis=1, tiled=True)]
    all_gather x1, waiting for transfers between devices: 47.2 us -> 0.01 us  [body(): right_whole = lax.all_gather(right_slab, 'row', axis=1, tiled=True)]
    all_gather x1, waiting for transfers between devices: 41.8 us -> 11.3 us  [body(): lax.all_gather(left_weight_slab, 'col', axis=1, tiled=True)]
    convert_element_type x0 -> x1, other arithmetic: none -> 10.2 us  [combine_blocks(): (2.0 * as_float - jnp.swapaxes(as_float, -1, -2)).astype(jnp.bfloat16)]
    all_to_all x0 -> x1, starting transfers between devices: none -> 6.36 us  [body(): lax.all_to_all(jnp.stack([left_slab] * lax.axis_size('col')), 'col', 0, 0)]
    all_gather x1, waiting for transfers between devices: 45.9 us -> 49.9 us  [body(): lax.all_gather(right_weight_slab, 'row', axis=1, tiled=True)]
    another operation x0 -> x1, local copies, waits for them, and re-layouts: none -> 3.59 us  [body(): jnp.stack([left_slab] * lax.axis_size('col'))]
  transfers between devices with their start and end apart: 4 -> 4, of which waited for: 4 -> 3; matrix products, arithmetic and copies ran while one was open for 16% -> 26% of each run, Pallas kernels for 0% -> 0%
where the time goes in v1:
time: 220 us; the launch traced here: 219 us
  waiting for transfers between devices  129 us (59%)
  matrix products  25.4 us (12%)
  other arithmetic  23.2 us (11%)
  local copies, waits for them, and re-layouts  21 us (10%)
  between operations  14.4 us (7%)
  starting transfers between devices  6.44 us (3%)
    all_to_all x1, waiting for transfers between devices, body(): lax.all_to_all(jnp.stack([left_slab] * lax.axis_size('col')), 'col', 0, 0)  65.3 us
    all_gather x1, waiting for transfers between devices, body(): lax.all_gather(right_weight_slab, 'row', axis=1, tiled=True)  49.9 us
    convert_element_type x2, local copies, waits for them, and re-layouts, combine_blocks(): as_float = blocks.astype(jnp.float32)  17.4 us
    convert_element_type x2, other arithmetic, combine_blocks(): as_float = blocks.astype(jnp.float32)  13 us
    dot_general x1, matrix products, body(): jnp.einsum('kac,kcb->ab', mixed_cols, lax.all_gather(right_weight_slab, '...  12.9 us
    dot_general x1, matrix products, body(): jnp.einsum('kac,kcb->ab', mixed_cols, lax.all_gather(left_weight_slab, 'c...  12.4 us
    all_gather x1, waiting for transfers between devices, body(): lax.all_gather(left_weight_slab, 'col', axis=1, tiled=True)  11.3 us
    convert_element_type x1, other arithmetic, combine_blocks(): (2.0 * as_float - jnp.swapaxes(as_float, -1, -2)).astype(jnp.bfloat16)  10.2 us
  transfers between devices with their start and end apart: 4, of which 3 were waited for; matrix products, arithmetic and copies ran while one was open for 26% of the time, Pallas kernels for 0%

profile of v1, /device:TPU:1, one launch (start us, length us, event | category | flops | bytes accessed | tf_op | source)
XLA Modules:
  0.0 219.0 jit_solution(3987838571597708899)
XLA Ops:
  6.5 0.0 all-gather.9.cloned.1.call-start
  6.5 0.7 all-gather.9.cloned.1.call-update
  7.3 0.0 all-gather.11.cloned.1.call-start
  7.3 0.7 all-gather.11.cloned.1.call-update
  8.0 3.6 %stack.3 = bf16[8,2,128,1024]{3,2,1,0:T(8,128)(2,1)} broadcast(bf16[2,128,1024]{2,1,0:T(8,128)(2,1)} %bitcast.49), dimensions={1,2,3} | broadcast | bytes 4718592 | tf_op jit(solution)/shard_map/stack | solution.py:27
  11.6 6.4 %all-to-all-start = ((bf16[8,2,128,1024]{3,2,1,0:T(8,128)(2,1)}), bf16[8,2,128,1024]{3,2,1,0:T(8,128)(2,1)}, u32[]{:S(2)}, u32[]{:S(2)}) async-start(bf16[8,2,128,1024]{3,2,1,0:T(8,128)(2,1)} %stack.3), calls=%async_computation | async-start | bytes 8388608 | tf_op jit(solution)/shard_map/all_to_all | solution.py:27
  18.0 0.0 all-gather.7.cloned.1.call-start
  18.0 0.7 all-gather.7.cloned.1.call-update
  20.0 65.3 %all-to-all-done = bf16[8,2,128,1024]{3,2,1,0:T(8,128)(2,1)} async-done(((bf16[8,2,128,1024]{3,2,1,0:T(8,128)(2,1)}), bf16[8,2,128,1024]{3,2,1,0:T(8,128)(2,1)}, u32[]{:S(2)}, u32[]{:S(2)}) %all-to-all-start) | async-done | bytes 4194336 | tf_op jit(solution)/shard_map/all_to_all | solution.py:27
  85.3 6.5 %copy_convert_fusion = f32[8,2,128,1024]{3,2,0,1:T(8,128)} fusion(bf16[8,2,128,1024]{3,2,1,0:T(8,128)(2,1)} %all-to-all-done), kind=kLoop, calls=%fused_computation.13 | loop fusion | flops 2097152 | bytes 12582912 | tf_op jit(solution)/shard_map/convert_element_type | solution.py:8
  91.8 8.7 %copy.24 = f32[2,1024,1024]{1,2,0:T(8,128)} copy(f32[2,1024,1024]{2,1,0:T(8,128)} %bitcast.48) | data formatting | bytes 16777216 | tf_op jit(solution)/shard_map/convert_element_type | solution.py:8
  100.4 10.2 %fusion = bf16[2,1024,1024]{1,2,0:T(8,128)(2,1)} fusion(f32[8,2,128,1024]{3,2,0,1:T(8,128)} %copy_convert_fusion, f32[2,1024,1024]{1,2,0:T(8,128)} %copy.24), kind=kLoop, calls=%fused_computation.1 | loop fusion | flops 6291456 | bytes 20971520 | tf_op jit(solution)/shard_map/convert_element_type | solution.py:9
  110.6 0.0 all-gather.9.cloned.1.call-done
  110.6 6.5 %bitcast_convert_fusion = f32[2,1024,1024]{2,1,0:T(8,128)} fusion(bf16[1,2,1024,1024]{3,2,1,0:T(8,128)(2,1)} %all-gather.9.cloned.1.call-done), kind=kLoop, calls=%fused_computation.10 | loop fusion | flops 2097152 | bytes 12582912 | tf_op jit(solution)/shard_map/convert_element_type | solution.py:8
  117.1 8.8 %copy.27 = f32[2,1024,1024]{1,2,0:T(8,128)} copy(f32[2,1024,1024]{2,1,0:T(8,128)} %bitcast_convert_fusion) | data formatting | bytes 16777216 | tf_op jit(solution)/shard_map/convert_element_type | solution.py:8
  125.9 0.0 copy-start
  125.9 11.3 %all-gather.11.cloned.1.call-done = bf16[2,1,1024,1024]{3,2,0,1:T(8,128)(2,1)} async-done(((bf16[2,1,128,1024]{3,2,0,1:T(8,128)(2,1)}), bf16[2,1,1024,1024]{3,2,0,1:T(8,128)(2,1)}) %all-gather.11.cloned.1.call-update) | async-done | bytes 4194320 | tf_op jit(solution)/shard_map/all_gather | solution.py:43
  137.2 12.4 %fusion.2 = f32[1024,1024,1]{0,1,2:T(8,128)} fusion(f32[2,1024,1024]{1,2,0:T(8,128)} %copy.27, bf16[2,1,1024,1024]{3,2,0,1:T(8,128)(2,1)} %all-gather.11.cloned.1.call-done, bf16[1,2,1024,1024]{3,2,1,0:T(8,128)(2,1)} %all-gather.9.cloned.1.call-done), kind=kOutput, calls=%fused_computation.4 | convolution fusion | flops 4303355904 | bytes 20971520 | tf_op jit(solution)/shard_map/kac,kcb->ab/dot_general | solution.py:40
  149.7 49.9 %all-gather.7.cloned.1.call-done = bf16[2,1,1024,1024]{3,2,0,1:T(8,128)(2,1)} async-done(((bf16[2,1,32,1024]{3,2,0,1:T(8,128)(2,1)}), bf16[2,1,1024,1024]{3,2,0,1:T(8,128)(2,1)}) %all-gather.7.cloned.1.call-update) | async-done | bytes 4194320 | tf_op jit(solution)/shard_map/all_gather | solution.py:34
  199.5 0.0 copy-done
  199.5 12.9 %fusion.6 = f32[1,1,1024,1024]{3,2,1,0:T(8,128)} fusion(f32[1024,1024,1]{0,1,2:T(8,128)} %fusion.2, f32[1,1,1024,1024]{3,2,1,0:T(8,128)} %param.8, f32[1024]{0:T(1024)S(1)} %copy-done, f32[]{:T(128)} %bitcast.16, bf16[2,1024,1024]{1,2,0:T(8,128)(2,1)} %fusion, bf16[2,1,1024,1024]{3,2,0,1:T(8,128)(2,1)} %all-gather.7.cloned.1.call-done), kind=kOutput, calls=%fused_computation.8 | convolution fusion | flops 4300210176 | bytes 20975620 | tf_op jit(solution)/shard_map/kac,kcb->ab/dot_general | solution.py:31
Async XLA Ops:
  6.5 104.1 %all-gather.9.cloned.1.call-start = ((), (), s32[]{:S(2)}) async-start(), calls=%async_computation.2 | async-start | bytes 4325376 | tf_op jit(solution)/shard_map/all_gather | solution.py:37
  7.3 130.0 %all-gather.11.cloned.1.call-start = ((), (), s32[]{:S(2)}) async-start(), calls=%async_computation.3 | async-start | bytes 4718592 | tf_op jit(solution)/shard_map/all_gather | solution.py:43
  11.6 73.7 %all-to-all-start = ((bf16[8,2,128,1024]{3,2,1,0:T(8,128)(2,1)}), bf16[8,2,128,1024]{3,2,1,0:T(8,128)(2,1)}, u32[]{:S(2)}, u32[]{:S(2)}) async-start(bf16[8,2,128,1024]{3,2,1,0:T(8,128)(2,1)} %stack.3), calls=%async_computation | async-start | bytes 8388608 | tf_op jit(solution)/shard_map/all_to_all | solution.py:27
  18.0 181.6 %all-gather.7.cloned.1.call-start = ((), (), s32[]{:S(2)}) async-start(), calls=%async_computation.1 | async-start | bytes 4325376 | tf_op jit(solution)/shard_map/all_gather | solution.py:34
  125.9 73.6 %copy-start = (f32[1024]{0:T(1024)S(1)}, f32[1024]{0:T(1024)}, u32[]{:S(2)}) copy-start(f32[1024]{0:T(1024)} %param.15) | copy-start | bytes 12292
Sparse Core Ops, SparseCore 0:
  10.0 73.0 all-gather.8
  84.9 52.2 all-gather.10
  139.9 59.5 all-gather.6
